TPU v7x, 32 devices: a whole 2x2x4 slice. The times are simulated.
32 devices in a mesh: dp: 16 (over z, x, core), head: 2 (over y).
Axes of the slice: x: 2, y: 2, z: 4, core: 2. Of those that a mesh axis runs over, the one named last changes fastest.
Arguments:
- layer_input: bfloat16 [16384, 768], P('dp', 'head'), may hold values from -6 to 6
- first_gain: float32 [768], replicated, may hold values from 0.5 to 1.5
- first_shift: float32 [768], replicated, may hold values from -3 to 3
- qkv_weight: bfloat16 [3, 768, 768], P(None, None, 'head'), may hold values from -0.5 to 0.5
- out_weight: bfloat16 [768, 768], P('head'), may hold values from -0.875 to 0.875
- second_gain: float32 [768], replicated, may hold values from 0.5 to 1.5
- second_shift: float32 [768], replicated, may hold values from -3 to 3
- up_weight: bfloat16 [768, 3072], P(None, 'head'), may hold values from -0.21875 to 0.21875
- down_weight: bfloat16 [3072, 768], P('head'), may hold values from -0.15625 to 0.15625
- segment_ids: int32 [16384], P('dp'), may hold values from 0 to 4, as said below
- pad_mask: int32 [16384], P('dp'), may hold values from 0 to 1, as said below
- cluster_ids: int32 [12, 16384], P('head', 'dp'), may hold values from 0 to 99, as said below
- output_grad: bfloat16 [16384, 768], P('dp', 'head'), may hold values from -6 to 6
Outputs:
- layer_output: bfloat16 [16384, 768], P('dp', 'head')
- input_grad: bfloat16 [16384, 768], P('dp', 'head')
- qkv_grad: float32 [3, 768, 768], P(None, None, 'head')
- mix_weight_grad: float32 [768, 768], P('head')
- up_grad: float32 [768, 3072], P(None, 'head')
- down_grad: float32 [3072, 768], P('head')
- first_gain_grad: float32 [768], replicated
- first_shift_grad: float32 [768], replicated
- second_gain_grad: float32 [768], replicated
- second_shift_grad: float32 [768], replicated
Inputs may be any that keep to these rules, and one draw needn't show every extreme that they name: `segment_ids`: never falling within a sequence of 1024 tokens; 4 documents numbered 0 .. 3, each of 128 tokens or more, then one or more padding tokens numbered 4 at the sequence's end. `pad_mask`: 1 exactly on the tokens of documents, 0 on padding. `cluster_ids`: in each head and sequence every cluster holds at least one token with pad_mask 1, and all such tokens of a cluster lie in one document.
All inputs are finite; a program needn't handle non-finite values.
Results may differ from a plain program's by a relative error of at most 0.015.
The roundings to bfloat16 on the way count: a program that leaves them out, or rounds other values in their place, can miss the bound.
Values may be sent and summed in bfloat16 or wider, within the bound.
A program may use at most 128 MiB of HBM per device.

v0:
```python
import jax
import jax.numpy as jnp
from jax import lax
from jax.sharding import PartitionSpec as P

HDIM = 64
CLUST = 100
epsilon = 1e-05
far_below = -1e30
highest = lax.Precision.HIGHEST


def norm_parts(values):
    row_mean = jnp.mean(values, axis=-1, keepdims=True)
    centred = values - row_mean
    variance = jnp.mean(centred * centred, axis=-1, keepdims=True)
    row_scale = lax.rsqrt(variance + epsilon)
    return (centred * row_scale, row_scale)


def norm_back(upstream, normal, row_scale):
    first_term = jnp.mean(upstream, axis=-1, keepdims=True)
    second_term = jnp.mean(upstream * normal, axis=-1, keepdims=True)
    return row_scale * (upstream - first_term - normal * second_term)


def attention_parts(query, keys, segment_ids, pad_mask, cluster_ids):
    live_rows = (pad_mask > 0).astype(jnp.float32)
    labels = jnp.arange(CLUST, dtype=jnp.int32)
    member = (cluster_ids[:, None, :] == labels[None, :, None]).astype(jnp.float32) * live_rows[
        None, None, :
    ]
    counts = jnp.sum(member, axis=-1)
    member_low = member.astype(jnp.bfloat16)
    centre = (
        jnp.einsum("hcs,she->hce", member_low, query, preferred_element_type=jnp.float32)
        / counts[:, :, None]
    ).astype(jnp.bfloat16)
    seg_float = segment_ids.astype(jnp.float32)
    doc_owner = jnp.einsum("hcs,s->hc", member, seg_float, precision=highest) / counts
    allowed = (jnp.abs(doc_owner[:, :, None] - seg_float[None, None, :]) < 0.5) & (
        pad_mask[None, None, :] > 0
    )
    scores = jnp.einsum(
        "hce,she->hcs", centre, keys, preferred_element_type=jnp.float32
    ) * HDIM ** (-0.5)
    masked = jnp.where(allowed, scores, far_below)
    return (member, member_low, counts, centre, masked)


def shards(
    layer_input,
    first_gain,
    first_shift,
    qkv_weight,
    out_weight,
    second_gain,
    second_shift,
    up_weight,
    down_weight,
    segment_ids,
    pad_mask,
    cluster_ids,
    output_grad,
):
    tokens, local_width = layer_input.shape
    head_count = cluster_ids.shape[0]
    score_scale = HDIM ** (-0.5)
    start = lax.axis_index("head") * local_width
    whole_in = lax.all_gather(layer_input, "head", axis=1, tiled=True).astype(jnp.float32)
    first_hat, first_scale = norm_parts(whole_in)
    normed = (first_hat * first_gain + first_shift).astype(jnp.bfloat16)
    projected = jnp.einsum(
        "td,ide->ite", normed, qkv_weight, preferred_element_type=jnp.float32
    ).astype(jnp.bfloat16)
    head_parts = projected.reshape(3, tokens, head_count, HDIM)
    query, keys, values = (head_parts[0], head_parts[1], head_parts[2])
    member, member_low, counts, centre, masked = attention_parts(
        query, keys, segment_ids, pad_mask, cluster_ids
    )
    row_top = jnp.max(masked, axis=-1, keepdims=True)
    log_total = row_top + jnp.log(jnp.sum(jnp.exp(masked - row_top), axis=-1, keepdims=True))
    weights = jnp.exp(masked - log_total).astype(jnp.bfloat16)
    centre_out = jnp.einsum(
        "hcs,she->hce", weights, values, preferred_element_type=jnp.float32
    ).astype(jnp.bfloat16)
    mixture = (
        jnp.einsum("hcs,hce->she", member_low, centre_out, preferred_element_type=jnp.float32)
        .astype(jnp.bfloat16)
        .reshape(tokens, local_width)
    )
    branch_part = jnp.dot(mixture, out_weight, preferred_element_type=jnp.float32)
    branch = lax.psum_scatter(
        branch_part.astype(jnp.bfloat16), "head", scatter_dimension=1, tiled=True
    ).astype(jnp.float32)
    residual = layer_input.astype(jnp.float32) + branch
    whole_res = lax.all_gather(residual.astype(jnp.bfloat16), "head", axis=1, tiled=True).astype(
        residual.dtype
    )
    second_hat, second_scale = norm_parts(whole_res)
    second = (second_hat * second_gain + second_shift).astype(jnp.bfloat16)
    hidden = jnp.dot(second, up_weight, preferred_element_type=jnp.float32)
    activated, gelu_back = jax.vjp(jax.nn.gelu, hidden)
    activated = activated.astype(jnp.bfloat16)
    ffn_part = jnp.dot(activated, down_weight, preferred_element_type=jnp.float32)
    ffn_out = lax.psum_scatter(
        ffn_part.astype(jnp.bfloat16), "head", scatter_dimension=1, tiled=True
    ).astype(jnp.float32)
    layer_output = (residual + ffn_out).astype(jnp.bfloat16)
    whole_grad = lax.all_gather(output_grad, "head", axis=1, tiled=True)
    down_grad = jnp.einsum("tf,td->fd", activated, whole_grad, preferred_element_type=jnp.float32)
    act_grad = jnp.einsum("td,fd->tf", whole_grad, down_weight, preferred_element_type=jnp.float32)
    hidden_grad = gelu_back(act_grad)[0].astype(jnp.bfloat16)
    up_grad = jnp.einsum("td,tf->df", second, hidden_grad, preferred_element_type=jnp.float32)
    second_part = jnp.einsum(
        "tf,df->td", hidden_grad, up_weight, preferred_element_type=jnp.float32
    )
    second_back = lax.psum(second_part, "head")
    second_gain_grad = jnp.sum(second_back * second_hat, axis=0)
    second_shift_grad = jnp.sum(second_back, axis=0)
    residual_grad = whole_grad.astype(jnp.float32) + norm_back(
        second_back * second_gain, second_hat, second_scale
    )
    branch_grad = residual_grad.astype(jnp.bfloat16)
    mix_weight_grad = jnp.einsum(
        "te,td->ed", mixture, branch_grad, preferred_element_type=jnp.float32
    )
    mixture_grad = jnp.einsum(
        "td,ed->te", branch_grad, out_weight, preferred_element_type=jnp.float32
    ).reshape(tokens, head_count, HDIM)
    centre_out_grad = jnp.einsum("hcs,she->hce", member, mixture_grad, precision=highest).astype(
        jnp.bfloat16
    )
    probs = jnp.exp(masked - log_total)
    prob_grad = jnp.einsum(
        "hce,she->hcs", centre_out_grad, values, preferred_element_type=jnp.float32
    )
    value_grad = jnp.einsum(
        "hcs,hce->she", weights, centre_out_grad, preferred_element_type=jnp.float32
    )
    score_grad = (probs * (prob_grad - jnp.sum(prob_grad * probs, axis=-1, keepdims=True))).astype(
        jnp.bfloat16
    )
    centre_grad = (
        jnp.einsum("hcs,she->hce", score_grad, keys, preferred_element_type=jnp.float32)
        * score_scale
    )
    key_grad = (
        jnp.einsum("hcs,hce->she", score_grad, centre, preferred_element_type=jnp.float32)
        * score_scale
    )
    query_grad = jnp.einsum(
        "hcs,hce->she", member, centre_grad / counts[:, :, None], precision=highest
    )
    proj_grad = (
        jnp.stack([query_grad, key_grad, value_grad])
        .reshape(3, tokens, local_width)
        .astype(jnp.bfloat16)
    )
    qkv_grad = jnp.einsum("td,ite->ide", normed, proj_grad, preferred_element_type=jnp.float32)
    first_part = jnp.einsum(
        "ite,ide->td", proj_grad, qkv_weight, preferred_element_type=jnp.float32
    )
    first_back = lax.psum(first_part.astype(jnp.bfloat16), "head").astype(jnp.float32)
    first_gain_grad = jnp.sum(first_back * first_hat, axis=0)
    first_shift_grad = jnp.sum(first_back, axis=0)
    input_full = residual_grad + norm_back(first_back * first_gain, first_hat, first_scale)
    input_grad = lax.dynamic_slice_in_dim(input_full, start, local_width, 1).astype(jnp.bfloat16)
    summed = lax.psum(
        (
            qkv_grad,
            mix_weight_grad,
            up_grad,
            down_grad,
            first_gain_grad,
            first_shift_grad,
            second_gain_grad,
            second_shift_grad,
        ),
        "dp",
    )
    (
        qkv_total,
        mix_total,
        up_total,
        down_total,
        first_gain_total,
        first_shift_total,
        second_gain_total,
        second_shift_total,
    ) = summed
    return (
        layer_output,
        input_grad,
        qkv_total,
        mix_total,
        up_total,
        down_total,
        first_gain_total,
        first_shift_total,
        second_gain_total,
        second_shift_total,
    )


def solution(mesh):
    placed = (
        P("dp", "head"),
        P(),
        P(),
        P(None, None, "head"),
        P("head", None),
        P(),
        P(),
        P(None, "head"),
        P("head", None),
        P("dp"),
        P("dp"),
        P("head", "dp"),
        P("dp", "head"),
    )
    return jax.shard_map(
        shards,
        mesh=mesh,
        in_specs=placed,
        out_specs=(
            P("dp", "head"),
            P("dp", "head"),
            P(None, None, "head"),
            P("head", None),
            P(None, "head"),
            P("head", None),
            P(),
            P(),
            P(),
            P(),
        ),
        check_vma=False,
    )
```

profile of v0, /device:TPU:0, one launch (start us, length us, event | category | flops | bytes accessed | tf_op | source)
XLA Modules:
  0.0 614.1 jit_solution(7935351262349309971)
XLA Ops:
  7.2 0.7 all-gather.4.cloned.1.call-update
  8.0 0.7 convert_element_type.94
  8.7 0.7 fusion.89
  9.4 1.1 select_reduce_fusion
  10.5 3.3 fusion.11
  13.8 25.7 %all-gather.4.cloned.1.call-done = bf16[1024,768]{1,0:T(8,128)(2,1)} async-done(((bf16[1024,384]{1,0:T(8,128)(2,1)}), bf16[1024,768]{1,0:T(8,128)(2,1)}) %all-gather.4.cloned.1.call-update) | async-done | bytes 1572880 | tf_op jit(solution)/shard_map/all_gather | solution.py:70
  39.5 1.8 convert_reduce_fusion.2
  41.4 0.6 fusion.29
  42.0 3.8 convert_bitcast_fusion
  46.1 0.5 copy-done.25
  46.6 0.6 fusion.62
  47.2 1.2 fusion.91
  48.4 1.5 copy-done.2
  49.8 0.7 exponential_reduce_fusion
  50.5 3.8 fusion.40
  54.3 3.5 convolution_convert_fusion
  57.8 2.6 copy.38
  60.4 0.7 all-gather.8.cloned.1.call-update
  61.1 25.5 %reduce-scatter.7.cloned.1.call-done = bf16[384,1024]{1,0:T(8,128)(2,1)} async-done(((bf16[768,1024]{1,0:T(8,128)(2,1)}), bf16[384,1024]{1,0:T(8,128)(2,1)}) %reduce-scatter.7.cloned.1.call-update) | async-done | bytes 786448
  86.7 2.3 copy.39
  89.0 2.2 fusion.39
  91.2 0.5 all-reduce.6.cloned.1.call-start
  91.7 23.7 %all-gather.8.cloned.1.call-done = bf16[1024,768]{1,0:T(8,128)(2,1)} async-done(((bf16[1024,384]{1,0:T(8,128)(2,1)}), bf16[1024,768]{1,0:T(8,128)(2,1)}) %all-gather.8.cloned.1.call-update) | async-done | bytes 1572880 | tf_op jit(solution)/shard_map/all_gather | solution.py:110
  115.4 7.4 %fusion.92 = f32[1024,1536]{1,0:T(8,128)} fusion(bf16[1024,768]{1,0:T(8,128)(2,1)} %all-gather.8.cloned.1.call-done, bf16[1536,768]{1,0:T(8,128)(2,1)} %param.21), kind=kOutput, calls=%fused_computation.127 | convolution fusion | flops 2415919104 | bytes 10223616 | tf_op jit(solution)/shard_map/td,fd->tf/dot_general | solution.py:112
  122.9 21.8 %all-gather.6.cloned.1.call-done = bf16[1024,768]{1,0:T(8,128)(2,1)} async-done(((bf16[1024,384]{1,0:T(8,128)(2,1)}), bf16[1024,768]{1,0:T(8,128)(2,1)}) %all-gather.6.cloned.1.call-update) | async-done | bytes 1572880 | tf_op jit(solution)/shard_map/all_gather | solution.py:97
  144.6 1.8 convert_reduce_fusion.1
  146.5 0.6 fusion.28
  147.2 9.7 %fusion.6 = (bf16[1024,1536]{1,0:T(8,128)(2,1)S(1)}, f32[1024,1536]{1,0:T(8,128)}) fusion(f32[1024,1536]{1,0:T(8,128)} %fusion.92, bf16[768,1536]{1,0:T(8,128)(2,1)S(1)} %copy-done, bf16[1024,768]{1,0:T(8,128)(2,1)S(1)} %copy-done.7, f32[768]{0:T(1024)S(1)} %copy-done.28, f32[768]{0:T(1024)S(1)} %copy-done.26, f32[1024]{0:T(1024)S(1)} %add_rsqrt_fusion, ...), kind=kOutput, calls=%fused_computation.8 | convolution fusion | flops 2452094976 | bytes 19675136 | tf_op jit(solution)/shard_map/dot_general | solution.py:102
  156.9 1.7 copy-done.30
  158.6 4.3 fusion.93
  163.0 7.2 %convolution_convert_fusion.1 = bf16[1024,768]{1,0:T(8,128)(2,1)S(1)} fusion(bf16[1536,768]{1,0:T(8,128)(2,1)} %param.21, f32[1024,1536]{1,0:T(8,128)} %get-tuple-element.56), kind=kOutput, calls=%fused_computation.60 | convolution fusion | flops 2430861312 | bytes 10223616 | tf_op jit(solution)/shard_map/dot_general | solution.py:105
  170.2 1.6 copy.40
  171.9 9.2 %fusion.86 = f32[1536,768]{1,0:T(8,128)} fusion(bf16[1024,768]{1,0:T(8,128)(2,1)} %all-gather.8.cloned.1.call-done, f32[1024,1536]{1,0:T(8,128)} %get-tuple-element.56), kind=kOutput, calls=%fused_computation.123 | convolution fusion | flops 2430074880 | bytes 12582912 | tf_op jit(solution)/shard_map/tf,td->fd/dot_general | solution.py:111
  181.1 67.8 %all-reduce.6.cloned.1.call-done = f32[1024,768]{1,0:T(8,128)} async-done(((f32[1024,768]{1,0:T(8,128)}), f32[1024,768]{1,0:T(8,128)}) %all-reduce.6.cloned.1.call-update) | async-done | bytes 3145744 | tf_op jit(solution)/shard_map/psum | solution.py:118
  248.9 3.4 fusion.27
  252.3 1.4 fusion.26
  253.8 0.8 fusion.68
  254.6 0.8 copy-done.5
  255.4 3.2 fusion.63
  258.7 0.7 convolution_convert_fusion.2
  259.4 1.2 copy.32
  260.6 2.8 multiply_reduce_fusion.2
  263.4 0.5 multiply_convert_fusion.1
  264.0 1.0 copy-done.14
  265.4 1.1 copy.31
  266.6 2.2 fusion.61
  268.8 2.7 fusion.41
  271.5 2.3 copy.30
  273.8 5.3 bitcast_convert_fusion
  279.2 6.8 %fusion.82 = f32[768,1536]{1,0:T(8,128)} fusion(bf16[1024,1536]{1,0:T(8,128)(2,1)} %copy-done.30, bf16[1024,768]{1,0:T(8,128)(2,1)S(1)} %copy-done.8, f32[768]{0:T(1024)S(1)} %copy-done.28, f32[768]{0:T(1024)S(1)} %copy-done.26, f32[1024]{0:T(1024)S(1)} %add_rsqrt_fusion, f32[1024]{0:T(1024)S(1)} %broadcast_multiply_fusion.4), kind=kOutput, calls=%fused_computation.121 | convolution fusion | flops 2420637696 | bytes 9451520 | tf_op jit(solution)/shard_map/td,tf->df/dot_general | solution.py:114
  286.1 1.8 fusion.66
  288.0 0.5 copy-done.23
  288.5 4.3 convolution_bitcast_fusion
  292.9 2.3 copy.41
  295.2 2.3 add_convert_fusion.1
  297.5 33.5 %all-reduce.8.cloned.1.call-done = bf16[1024,768]{1,0:T(8,128)(2,1)} async-done(((bf16[1024,768]{1,0:T(8,128)(2,1)}), bf16[1024,768]{1,0:T(8,128)(2,1)}) %all-reduce.8.cloned.1.call-update) | async-done | bytes 1572880 | tf_op jit(solution)/shard_map/psum | solution.py:164
  331.0 4.6 fusion.30
  335.6 64.1 %all-reduce = (f32[768]{0:T(1024)}, f32[768]{0:T(1024)}, f32[768]{0:T(1024)}, f32[768]{0:T(1024)}) all-reduce(f32[768]{0:T(1024)S(1)} %get-tuple-element.32, f32[768]{0:T(1024)S(1)} %get-tuple-element.37, f32[768]{0:T(1024)S(1)} %get-tuple-element.30, f32[768]{0:T(1024)S(1)} %get-tuple-element.35), channel_id=1, replica_groups=mesh['dp'=16,'head'=2] {'dp'}, use_global_device_ids=true, to_apply=%region_21.22 | all-reduce | flops 3072 | bytes 24576 | tf_op jit(solution)/shard_map/psum | solution.py:169
  399.7 3.8 fusion.36
  403.4 189.6 %all-reduce.10.cloned.1.call-done = (f32[3,768,384]{1,2,0:T(8,128)}, f32[384,768]{1,0:T(8,128)}, f32[768,1536]{1,0:T(8,128)}, f32[1536,768]{1,0:T(8,128)}) async-done(((f32[3,768,384]{1,2,0:T(8,128)}, f32[384,768]{1,0:T(8,128)}, f32[768,1536]{1,0:T(8,128)}, f32[1536,768]{1,0:T(8,128)}), (f32[3,768,384]{1,2,0:T(8,128)}, f32[384,768]{1,0:T(8,128)}, f32[768,1536]{1,0:T(8,128)}, ...) | async-done | bytes 14155792 | tf_op jit(solution)/shard_map/psum | solution.py:169
  593.0 5.2 copy.34
  598.3 1.0 copy.49
  599.3 5.5 copy.50
  604.8 2.2 copy.51
  (86 shorter events, 1.5 us)
Async XLA Ops:
  7.2 140.0 %copy-start = (bf16[768,1536]{1,0:T(8,128)(2,1)S(1)}, bf16[768,1536]{1,0:T(8,128)(2,1)}, u32[]{:S(2)}) copy-start(bf16[768,1536]{1,0:T(8,128)(2,1)} %param.20) | copy-start | bytes 7077892
  7.2 32.3 %all-gather.4.cloned.1.call-start = ((), (), s32[]{:S(2)}) async-start(), calls=%async_computation.2 | async-start | bytes 2359296 | tf_op jit(solution)/shard_map/all_gather | solution.py:70
  7.9 34.1 %copy-start.27 = (f32[768]{0:T(1024)S(1)}, f32[768]{0:T(1024)}, u32[]{:S(2)}) copy-start(f32[768]{0:T(1024)} %param.14) | copy-start | bytes 9220
  7.9 34.1 %copy-start.29 = (f32[768]{0:T(1024)S(1)}, f32[768]{0:T(1024)}, u32[]{:S(2)}) copy-start(f32[768]{0:T(1024)} %param.15) | copy-start | bytes 9220
  7.9 78.7 %reduce-scatter.7.cloned.1.call-start = ((), (), s32[]{:S(2)}) async-start(), calls=%async_computation.7 | async-start | bytes 2359296
  39.5 1.9 copy-start.9
  45.8 0.8 copy-start.25
  46.1 2.3 copy-start.19
  46.1 4.4 copy-start.15
  48.3 1.5 copy-start.2
  60.3 28.6 %copy-start.12 = (bf16[1024,384]{1,0:T(8,128)(2,1)S(1)}, bf16[1024,384]{1,0:T(8,128)(2,1)}, u32[]{:S(2)}) copy-start(bf16[1024,384]{1,0:T(8,128)(2,1)} %param.13) | copy-start | bytes 2359300
  60.4 55.1 %all-gather.8.cloned.1.call-start = ((), (), s32[]{:S(2)}) async-start(), calls=%async_computation.4 | async-start | bytes 2359296 | tf_op jit(solution)/shard_map/all_gather | solution.py:110
  61.1 83.5 %all-gather.6.cloned.1.call-start = ((), (), s32[]{:S(2)}) async-start(), calls=%async_computation.3 | async-start | bytes 2359296 | tf_op jit(solution)/shard_map/all_gather | solution.py:97
  91.2 157.7 %all-reduce.6.cloned.1.call-start = ((), (), s32[]{:S(2)}) async-start(), calls=%async_computation.5 | async-start | bytes 6291456 | tf_op jit(solution)/shard_map/psum | solution.py:118
  122.9 24.3 %copy-start.26 = (f32[768]{0:T(1024)S(1)}, f32[768]{0:T(1024)}, u32[]{:S(2)}) copy-start(f32[768]{0:T(1024)} %param.18) | copy-start | bytes 9220
  122.9 24.3 %copy-start.28 = (f32[768]{0:T(1024)S(1)}, f32[768]{0:T(1024)}, u32[]{:S(2)}) copy-start(f32[768]{0:T(1024)} %param.19) | copy-start | bytes 9220
  144.6 1.9 copy-start.7
  156.9 1.7 copy-start.30
  162.9 129.9 %reduce-scatter.9.cloned.1.call-start = ((), (), s32[]{:S(2)}) async-start(), calls=%async_computation.8 | async-start | bytes 2359296
  171.9 77.0 %copy-start.8 = (bf16[1024,768]{1,0:T(8,128)(2,1)S(1)}, bf16[1024,768]{1,0:T(8,128)(2,1)}, u32[]{:S(2)}) copy-start(bf16[1024,768]{1,0:T(8,128)(2,1)} %all-gather.6.cloned.1.call-done) | copy-start | bytes 4718596
  171.9 159.1 %all-reduce.8.cloned.1.call-start = ((), (), s32[]{:S(2)}) async-start(), calls=%async_computation.6 | async-start | bytes 3145728 | tf_op jit(solution)/shard_map/psum | solution.py:164
  248.9 3.4 copy-start.11
  248.9 3.4 copy-start.16
  252.3 1.4 copy-start.24
  253.8 1.6 copy-start.5
  255.4 3.3 copy-start.3
  260.6 2.8 copy-start.4
  264.0 1.0 copy-start.14
  266.6 7.2 %copy-start.20 = (bf16[1,1024,384]{2,1,0:T(8,128)(2,1)S(1)}, bf16[1,1024,384]{2,1,0:T(8,128)(2,1)}, u32[]{:S(2)}) copy-start(bf16[1,1024,384]{2,1,0:T(8,128)(2,1)} %copy.32) | copy-start | bytes 2359300
  279.1 6.9 %copy-start.18 = (bf16[6,64,1024]{2,1,0:T(8,128)(2,1)S(1)}, bf16[6,64,1024]{2,1,0:T(8,128)(2,1)}, u32[]{:S(2)}) copy-start(bf16[6,64,1024]{2,1,0:T(8,128)(2,1)} %fusion.40) | copy-start | bytes 2359300
  279.1 313.9 %all-reduce.10.cloned.1.call-start = ((), (), s32[]{:S(2)}) async-start(), calls=%async_computation.9 | async-start | bytes 28311552 | tf_op jit(solution)/shard_map/psum | solution.py:169
  279.2 6.8 %copy-start.6 = (f32[1024,768]{1,0:T(8,128)S(1)}, f32[1024,768]{1,0:T(8,128)}, u32[]{:S(2)}) copy-start(f32[1024,768]{1,0:T(8,128)} %copy-done.5) | copy-start | bytes 9437188
  286.0 1.9 copy-start.10
  286.0 1.9 copy-start.21
  286.0 2.0 copy-start.22
  286.0 2.5 copy-start.23
  292.8 2.4 copy-start.13
  593.0 5.3 copy-start.17
  598.3 6.5 %slice-start = ((s8[4718592]{0:T(1024)(128)(4,1)}), s8[4194304]{0:T(1024)(128)(4,1)S(1)}, s32[]{:S(2)}) async-start(s8[4718592]{0:T(1024)(128)(4,1)} %bitcast.63), calls=%async_computation.10 | async-start | bytes 8388608
  599.3 5.5 slice-start.1
  599.3 7.7 %copy-start.1 = (bf16[768,1536]{1,0:T(8,128)(2,1)S(1)}, bf16[768,1536]{1,0:T(8,128)(2,1)}, u32[]{:S(2)}) copy-start(bf16[768,1536]{1,0:T(8,128)(2,1)} %param.20) | copy-start | bytes 7077892
Sparse Core Ops, SparseCore 0:
  9.5 29.9 all-gather.3
  60.5 26.1 reduce-scatter.6
  88.2 27.1 all-gather.7
  117.4 27.1 all-gather.5
  163.0 85.8 all-reduce.5
  251.0 26.1 reduce-scatter.8
  279.5 51.5 all-reduce.7
  336.2 256.7 all-reduce.9
where the time goes:
time: 623 us; the launch traced here: 614 us
  waiting for transfers between devices  389 us (62%)
  matrix products  85.2 us (14%)
  blocking collectives  64.1 us (10%)
  local copies, waits for them, and re-layouts  34.1 us (5%)
  other arithmetic  26.2 us (4%)
  between operations  14.8 us (2%)
    psum x1, waiting for transfers between devices, shards(): lax.psum((qkv_grad, mix_weight_grad, up_grad, down_grad, first_gain_grad,...  190 us
    psum x1, waiting for transfers between devices, shards(): second_back = lax.psum(second_part, 'head')  67.8 us
    psum x1, blocking collectives, shards(): lax.psum((qkv_grad, mix_weight_grad, up_grad, down_grad, first_gain_grad,...  64.1 us
    psum x1, waiting for transfers between devices, shards(): lax.psum(first_part.astype(jnp.bfloat16), 'head').astype(jnp.float32)  33.5 us
    unnamed x74, local copies, waits for them, and re-layouts  29.2 us
    unnamed x10, waiting for transfers between devices  27 us
    all_gather x1, waiting for transfers between devices, shards(): lax.all_gather(layer_input, 'head', axis=1, tiled=True).astype(jnp.float32)  25.7 us
    all_gather x1, waiting for transfers between devices, shards(): whole_grad = lax.all_gather(output_grad, 'head', axis=1, tiled=True)  23.7 us
  transfers between devices with their start and end apart: 8, of which 7 were waited for; matrix products, arithmetic and copies ran while one was open for 15% of the time, Pallas kernels for 0%

commit v1 on v0

--- a/solution.py
+++ b/solution.py
@@ -161,7 +161,9 @@
     first_part = jnp.einsum(
         "ite,ide->td", proj_grad, qkv_weight, preferred_element_type=jnp.float32
     )
-    first_back = lax.psum(first_part.astype(jnp.bfloat16), "head").astype(jnp.float32)
+    first_back = jnp.sum(lax.all_gather(first_part.astype(jnp.bfloat16), "head"), axis=0).astype(
+        jnp.float32
+    )
     first_gain_grad = jnp.sum(first_back * first_hat, axis=0)
     first_shift_grad = jnp.sum(first_back, axis=0)
     input_full = residual_grad + norm_back(first_back * first_gain, first_hat, first_scale)

time: 623 us -> 616 us (0.989)
  waiting for transfers between devices: 389 us -> 374 us
    psum x1 -> x0, waiting for transfers between devices: 33.5 us -> none  [shards(): lax.psum(first_part.astype(jnp.bfloat16), 'head').astype(jnp.float32)]
    all_gather x0 -> x1, waiting for transfers between devices: none -> 17.3 us  [shards(): lax.all_gather(first_part.astype(jnp.bfloat16), 'head')]
    unnamed x74 -> x78, local copies, waits for them, and re-layouts: 29.2 us -> 32 us
  transfers between devices with their start and end apart: 8 -> 8, of which waited for: 7 -> 7; matrix products, arithmetic and copies ran while one was open for 15% -> 16% of each run, Pallas kernels for 0% -> 0%
where the time goes in v1:
time: 616 us; the launch traced here: 607 us
  waiting for transfers between devices  374 us (61%)
  matrix products  85.5 us (14%)
  blocking collectives  64.3 us (10%)
  local copies, waits for them, and re-layouts  36.8 us (6%)
  other arithmetic  30.1 us (5%)
  between operations  14.8 us (2%)
    psum x1, waiting for transfers between devices, shards(): lax.psum((qkv_grad, mix_weight_grad, up_grad, down_grad, first_gain_grad,...  185 us
    psum x1, waiting for transfers between devices, shards(): second_back = lax.psum(second_part, 'head')  73.7 us
    psum x1, blocking collectives, shards(): lax.psum((qkv_grad, mix_weight_grad, up_grad, down_grad, first_gain_grad,...  64.3 us
    unnamed x78, local copies, waits for them, and re-layouts  32 us
    unnamed x10, waiting for transfers between devices  27 us
    all_gather x1, waiting for transfers between devices, shards(): lax.all_gather(layer_input, 'head', axis=1, tiled=True).astype(jnp.float32)  25.7 us
    all_gather x1, waiting for transfers between devices, shards(): whole_grad = lax.all_gather(output_grad, 'head', axis=1, tiled=True)  23.7 us
    all_gather x1, waiting for transfers between devices, shards(): lax.all_gather(residual.astype(jnp.bfloat16), 'head', axis=1, tiled=True)  21.8 us
  transfers between devices with their start and end apart: 8, of which 7 were waited for; matrix products, arithmetic and copies ran while one was open for 16% of the time, Pallas kernels for 0%

profile of v1, /device:TPU:0, one launch (start us, length us, event | category | flops | bytes accessed | tf_op | source)
XLA Modules:
  0.0 607.1 jit_solution(6822943436890923195)
XLA Ops:
  7.2 0.7 all-gather.6.cloned.1.call-update
  8.0 0.7 convert_element_type.96
  8.7 0.7 fusion.89
  9.4 1.1 select_reduce_fusion
  10.5 3.3 fusion.11
  13.8 25.7 %all-gather.6.cloned.1.call-done = bf16[1024,768]{1,0:T(8,128)(2,1)} async-done(((bf16[1024,384]{1,0:T(8,128)(2,1)}), bf16[1024,768]{1,0:T(8,128)(2,1)}) %all-gather.6.cloned.1.call-update) | async-done | bytes 1572880 | tf_op jit(solution)/shard_map/all_gather | solution.py:70
  39.5 1.8 convert_reduce_fusion.2
  41.4 0.6 fusion.29
  42.0 3.8 convert_bitcast_fusion
  46.1 0.5 copy-done.26
  46.6 0.6 fusion.62
  47.2 1.2 fusion.91
  48.4 1.5 copy-done.2
  49.8 0.7 exponential_reduce_fusion
  50.5 3.8 fusion.40
  54.3 3.5 convolution_convert_fusion
  57.8 2.6 copy.38
  60.4 0.7 all-gather.10.cloned.1.call-update
  61.1 25.5 %reduce-scatter.7.cloned.1.call-done = bf16[384,1024]{1,0:T(8,128)(2,1)} async-done(((bf16[768,1024]{1,0:T(8,128)(2,1)}), bf16[384,1024]{1,0:T(8,128)(2,1)}) %reduce-scatter.7.cloned.1.call-update) | async-done | bytes 786448
  86.7 2.3 copy.39
  89.0 2.2 fusion.39
  91.7 23.7 %all-gather.10.cloned.1.call-done = bf16[1024,768]{1,0:T(8,128)(2,1)} async-done(((bf16[1024,384]{1,0:T(8,128)(2,1)}), bf16[1024,768]{1,0:T(8,128)(2,1)}) %all-gather.10.cloned.1.call-update) | async-done | bytes 1572880 | tf_op jit(solution)/shard_map/all_gather | solution.py:110
  115.4 7.4 %fusion.92 = f32[1024,1536]{1,0:T(8,128)} fusion(bf16[1024,768]{1,0:T(8,128)(2,1)} %all-gather.10.cloned.1.call-done, bf16[1536,768]{1,0:T(8,128)(2,1)} %param.21), kind=kOutput, calls=%fused_computation.127 | convolution fusion | flops 2415919104 | bytes 10223616 | tf_op jit(solution)/shard_map/td,fd->tf/dot_general | solution.py:112
  122.9 21.8 %all-gather.8.cloned.1.call-done = bf16[1024,768]{1,0:T(8,128)(2,1)} async-done(((bf16[1024,384]{1,0:T(8,128)(2,1)}), bf16[1024,768]{1,0:T(8,128)(2,1)}) %all-gather.8.cloned.1.call-update) | async-done | bytes 1572880 | tf_op jit(solution)/shard_map/all_gather | solution.py:97
  144.6 1.8 convert_reduce_fusion.1
  146.5 0.6 fusion.28
  147.2 9.7 %fusion.6 = (bf16[1024,1536]{1,0:T(8,128)(2,1)S(1)}, f32[1024,1536]{1,0:T(8,128)}) fusion(f32[1024,1536]{1,0:T(8,128)} %fusion.92, bf16[768,1536]{1,0:T(8,128)(2,1)S(1)} %copy-done, bf16[1024,768]{1,0:T(8,128)(2,1)S(1)} %copy-done.7, f32[768]{0:T(1024)S(1)} %copy-done.30, f32[768]{0:T(1024)S(1)} %copy-done.27, f32[1024]{0:T(1024)S(1)} %add_rsqrt_fusion, ...), kind=kOutput, calls=%fused_computation.8 | convolution fusion | flops 2452094976 | bytes 19675136 | tf_op jit(solution)/shard_map/dot_general | solution.py:102
  156.9 1.7 copy-done.32
  158.6 4.3 fusion.93
  162.9 1.6 copy-done.29
  164.5 7.7 %convolution_convert_fusion.1 = bf16[1024,768]{1,0:T(8,128)(2,1)} fusion(bf16[1536,768]{1,0:T(8,128)(2,1)S(1)} %copy-done.29, f32[1024,1536]{1,0:T(8,128)} %get-tuple-element.56), kind=kOutput, calls=%fused_computation.60 | convolution fusion | flops 2430861312 | bytes 10223616 | tf_op jit(solution)/shard_map/dot_general | solution.py:105
  172.2 2.7 copy.40
  175.2 73.7 %all-reduce.5.cloned.1.call-done = f32[1024,768]{1,0:T(8,128)} async-done(((f32[1024,768]{1,0:T(8,128)}), f32[1024,768]{1,0:T(8,128)}) %all-reduce.5.cloned.1.call-update) | async-done | bytes 3145744 | tf_op jit(solution)/shard_map/psum | solution.py:118
  248.9 3.2 fusion.27
  252.2 1.4 fusion.26
  253.6 0.8 fusion.68
  254.4 0.8 copy-done.5
  255.2 3.2 fusion.63
  258.5 0.7 convolution_convert_fusion.2
  259.2 1.2 copy.32
  260.4 2.8 multiply_reduce_fusion.2
  263.2 0.5 multiply_convert_fusion.1
  263.8 1.0 copy-done.14
  265.2 1.2 copy.31
  266.4 2.2 fusion.61
  268.5 2.7 fusion.41
  271.3 2.3 copy.30
  273.6 5.4 bitcast_convert_fusion
  279.2 6.6 %fusion.82 = f32[768,1536]{1,0:T(8,128)} fusion(bf16[1024,1536]{1,0:T(8,128)(2,1)} %copy-done.32, bf16[1024,768]{1,0:T(8,128)(2,1)S(1)} %copy-done.8, f32[768]{0:T(1024)S(1)} %copy-done.30, f32[768]{0:T(1024)S(1)} %copy-done.27, f32[1024]{0:T(1024)S(1)} %add_rsqrt_fusion, f32[1024]{0:T(1024)S(1)} %broadcast_multiply_fusion.4), kind=kOutput, calls=%fused_computation.121 | convolution fusion | flops 2420637696 | bytes 9451520 | tf_op jit(solution)/shard_map/td,tf->df/dot_general | solution.py:114
  285.8 9.4 %fusion.86 = f32[1536,768]{1,0:T(8,128)} fusion(bf16[1024,768]{1,0:T(8,128)(2,1)S(1)} %copy-done.17, f32[1024,1536]{1,0:T(8,128)} %get-tuple-element.56), kind=kOutput, calls=%fused_computation.123 | convolution fusion | flops 2430074880 | bytes 12582912 | tf_op jit(solution)/shard_map/tf,td->fd/dot_general | solution.py:111
  295.2 1.8 fusion.66
  297.7 4.3 convolution_bitcast_fusion
  302.0 2.3 copy.41
  304.4 2.3 add_convert_fusion.1
  306.7 17.3 %all-gather.12.cloned.1.call-done = bf16[2048,768]{1,0:T(8,128)(2,1)} async-done(((bf16[1024,768]{1,0:T(8,128)(2,1)}), bf16[2048,768]{1,0:T(8,128)(2,1)}) %all-gather.12.cloned.1.call-update) | async-done | bytes 3145744 | tf_op jit(solution)/shard_map/all_gather | solution.py:164
  324.0 4.1 reduce_sum.156
  328.1 4.6 fusion.30
  332.7 64.3 %all-reduce = (f32[768]{0:T(1024)}, f32[768]{0:T(1024)}, f32[768]{0:T(1024)}, f32[768]{0:T(1024)}) all-reduce(f32[768]{0:T(1024)S(1)} %get-tuple-element.32, f32[768]{0:T(1024)S(1)} %get-tuple-element.37, f32[768]{0:T(1024)S(1)} %get-tuple-element.30, f32[768]{0:T(1024)S(1)} %get-tuple-element.35), channel_id=1, replica_groups=mesh['dp'=16,'head'=2] {'dp'}, use_global_device_ids=true, to_apply=%region_21.22 | all-reduce | flops 3072 | bytes 24576 | tf_op jit(solution)/shard_map/psum | solution.py:171
  397.0 3.8 fusion.36
  400.8 185.2 %all-reduce.7.cloned.1.call-done = (f32[3,768,384]{1,2,0:T(8,128)}, f32[384,768]{1,0:T(8,128)}, f32[768,1536]{1,0:T(8,128)}, f32[1536,768]{1,0:T(8,128)}) async-done(((f32[3,768,384]{1,2,0:T(8,128)}, f32[384,768]{1,0:T(8,128)}, f32[768,1536]{1,0:T(8,128)}, f32[1536,768]{1,0:T(8,128)}), (f32[3,768,384]{1,2,0:T(8,128)}, f32[384,768]{1,0:T(8,128)}, f32[768,1536]{1,0:T(8,128)}, ...) | async-done | bytes 14155792 | tf_op jit(solution)/shard_map/psum | solution.py:171
  586.0 5.2 copy.34
  591.3 1.0 copy.48
  592.3 5.5 copy.49
  597.8 2.2 copy.50
  (91 shorter events, 2.9 us)
Async XLA Ops:
  7.2 140.0 %copy-start = (bf16[768,1536]{1,0:T(8,128)(2,1)S(1)}, bf16[768,1536]{1,0:T(8,128)(2,1)}, u32[]{:S(2)}) copy-start(bf16[768,1536]{1,0:T(8,128)(2,1)} %param.20) | copy-start | bytes 7077892
  7.2 32.3 %all-gather.6.cloned.1.call-start = ((), (), s32[]{:S(2)}) async-start(), calls=%async_computation.2 | async-start | bytes 2359296 | tf_op jit(solution)/shard_map/all_gather | solution.py:70
  7.9 34.1 %copy-start.28 = (f32[768]{0:T(1024)S(1)}, f32[768]{0:T(1024)}, u32[]{:S(2)}) copy-start(f32[768]{0:T(1024)} %param.14) | copy-start | bytes 9220
  7.9 34.1 %copy-start.31 = (f32[768]{0:T(1024)S(1)}, f32[768]{0:T(1024)}, u32[]{:S(2)}) copy-start(f32[768]{0:T(1024)} %param.15) | copy-start | bytes 9220
  7.9 78.7 %reduce-scatter.7.cloned.1.call-start = ((), (), s32[]{:S(2)}) async-start(), calls=%async_computation.7 | async-start | bytes 2359296
  39.5 1.9 copy-start.9
  45.8 0.8 copy-start.26
  46.1 2.3 copy-start.20
  46.1 4.4 copy-start.15
  48.3 1.5 copy-start.2
  60.3 28.6 %copy-start.12 = (bf16[1024,384]{1,0:T(8,128)(2,1)S(1)}, bf16[1024,384]{1,0:T(8,128)(2,1)}, u32[]{:S(2)}) copy-start(bf16[1024,384]{1,0:T(8,128)(2,1)} %param.13) | copy-start | bytes 2359300
  60.4 55.1 %all-gather.10.cloned.1.call-start = ((), (), s32[]{:S(2)}) async-start(), calls=%async_computation.4 | async-start | bytes 2359296 | tf_op jit(solution)/shard_map/all_gather | solution.py:110
  61.1 83.5 %all-gather.8.cloned.1.call-start = ((), (), s32[]{:S(2)}) async-start(), calls=%async_computation.3 | async-start | bytes 2359296 | tf_op jit(solution)/shard_map/all_gather | solution.py:97
  91.2 157.7 %all-reduce.5.cloned.1.call-start = ((), (), s32[]{:S(2)}) async-start(), calls=%async_computation.5 | async-start | bytes 6291456 | tf_op jit(solution)/shard_map/psum | solution.py:118
  122.9 24.3 %copy-start.27 = (f32[768]{0:T(1024)S(1)}, f32[768]{0:T(1024)}, u32[]{:S(2)}) copy-start(f32[768]{0:T(1024)} %param.18) | copy-start | bytes 9220
  122.9 24.3 %copy-start.30 = (f32[768]{0:T(1024)S(1)}, f32[768]{0:T(1024)}, u32[]{:S(2)}) copy-start(f32[768]{0:T(1024)} %param.19) | copy-start | bytes 9220
  144.6 1.9 copy-start.7
  156.9 1.7 copy-start.32
  162.9 1.7 copy-start.29
  162.9 139.1 %reduce-scatter.9.cloned.1.call-start = ((), (), s32[]{:S(2)}) async-start(), calls=%async_computation.8 | async-start | bytes 2359296
  172.2 76.6 %copy-start.8 = (bf16[1024,768]{1,0:T(8,128)(2,1)S(1)}, bf16[1024,768]{1,0:T(8,128)(2,1)}, u32[]{:S(2)}) copy-start(bf16[1024,768]{1,0:T(8,128)(2,1)} %all-gather.8.cloned.1.call-done) | copy-start | bytes 4718596
  175.0 149.1 %all-gather.12.cloned.1.call-start = ((), (), s32[]{:S(2)}) async-start(), calls=%async_computation.6 | async-start | bytes 4718592 | tf_op jit(solution)/shard_map/all_gather | solution.py:164
  248.9 3.2 copy-start.11
  248.9 3.3 copy-start.16
  252.2 1.4 copy-start.25
  253.6 1.7 copy-start.5
  255.2 3.3 copy-start.3
  260.4 2.8 copy-start.4
  263.8 1.0 copy-start.14
  266.4 7.2 %copy-start.21 = (bf16[1,1024,384]{2,1,0:T(8,128)(2,1)S(1)}, bf16[1,1024,384]{2,1,0:T(8,128)(2,1)}, u32[]{:S(2)}) copy-start(bf16[1,1024,384]{2,1,0:T(8,128)(2,1)} %copy.32) | copy-start | bytes 2359300
  278.9 307.1 %all-reduce.7.cloned.1.call-start = ((), (), s32[]{:S(2)}) async-start(), calls=%async_computation.9 | async-start | bytes 28311552 | tf_op jit(solution)/shard_map/psum | solution.py:171
  279.2 6.6 %copy-start.17 = (bf16[1024,768]{1,0:T(8,128)(2,1)S(1)}, bf16[1024,768]{1,0:T(8,128)(2,1)}, u32[]{:S(2)}) copy-start(bf16[1024,768]{1,0:T(8,128)(2,1)} %all-gather.10.cloned.1.call-done) | copy-start | bytes 4718596
  285.8 9.4 %copy-start.6 = (f32[1024,768]{1,0:T(8,128)S(1)}, f32[1024,768]{1,0:T(8,128)}, u32[]{:S(2)}) copy-start(f32[1024,768]{1,0:T(8,128)} %copy-done.5) | copy-start | bytes 9437188
  285.8 9.4 %copy-start.19 = (bf16[6,64,1024]{2,1,0:T(8,128)(2,1)S(1)}, bf16[6,64,1024]{2,1,0:T(8,128)(2,1)}, u32[]{:S(2)}) copy-start(bf16[6,64,1024]{2,1,0:T(8,128)(2,1)} %fusion.40) | copy-start | bytes 2359300
  295.2 1.8 copy-start.10
  295.2 1.8 copy-start.22
  295.2 2.1 copy-start.23
  295.2 2.5 copy-start.24
  302.0 2.4 copy-start.13
  586.0 5.3 copy-start.18
  591.3 6.5 %slice-start = ((s8[4718592]{0:T(1024)(128)(4,1)}), s8[4194304]{0:T(1024)(128)(4,1)S(1)}, s32[]{:S(2)}) async-start(s8[4718592]{0:T(1024)(128)(4,1)} %bitcast.64), calls=%async_computation.10 | async-start | bytes 8388608
  592.3 5.5 slice-start.1
  592.3 7.7 %copy-start.1 = (bf16[768,1536]{1,0:T(8,128)(2,1)S(1)}, bf16[768,1536]{1,0:T(8,128)(2,1)}, u32[]{:S(2)}) copy-start(bf16[768,1536]{1,0:T(8,128)(2,1)} %param.20) | copy-start | bytes 7077892
Sparse Core Ops, SparseCore 0:
  9.5 29.9 all-gather.5
  60.5 26.1 reduce-scatter.6
  88.2 27.1 all-gather.9
  117.4 27.1 all-gather.7
  163.0 85.7 all-reduce.4
  251.0 26.1 reduce-scatter.8
  279.1 44.8 all-gather.11
  329.2 256.8 all-reduce.6
